TPU v7x, 32 devices: a whole 2x2x4 slice. The times are simulated.
32 devices in a mesh: grp: 4 (over z), row: 4 (over x, core), col: 2 (over y).
Axes of the slice: x: 2, y: 2, z: 4, core: 2. Of those that a mesh axis runs over, the one named last changes fastest.
Arguments:
- acts: bfloat16 [768, 8192], P('grp', 'col'), may hold values from -6 to 6
- grads: bfloat16 [768, 28672], P('grp', ('row', 'col')), may hold values from -6 to 6
- basis_in: bfloat16 [8192, 4096], P('col', 'row'), may hold values from -0.0625 to 0.0625
- basis_out: bfloat16 [4, 7168, 14336], P('row', 'grp', 'col'), may hold values from -0.03125 to 0.03125
- lengths: int32 [4, 2], P('grp'), may hold values from 1 to 96, 144 in all within a row
Outputs:
- eigenvalues: float32 [14336, 4096], P('col', 'row')
Inputs may be any that keep to these rules, and one draw needn't show every extreme that they name: The 2 lengths of each index of grp sum to exactly 144, and none exceeds 96.
All inputs are finite; a program needn't handle non-finite values.
Results may differ from a plain program's by a relative error of at most 0.006.
Values may be sent and summed in bfloat16 or wider, within the bound.
A program may use at most 256 MiB of HBM per device.

v0:
```python
import jax
import jax.numpy as jnp
from jax import lax
from jax.sharding import PartitionSpec as P

LEN = 96
VALID = 144


def outer_square(left, right):
    block = lax.dot_general(
        left, right, (((0,), (0,)), ((), ())), preferred_element_type=jnp.float32
    )
    return block * block


def per_device(acts, grads, basis_in, basis_out, lengths):
    seq_lens = lengths[0]
    count = seq_lens.shape[0]
    partial_in = jnp.dot(acts, basis_in, preferred_element_type=jnp.float32)
    proj_in = lax.psum(partial_in, "col").astype(jnp.bfloat16)
    ends = jnp.cumsum(seq_lens)
    starts = ends - seq_lens
    slot_ids = jnp.arange(VALID, dtype=jnp.int32)
    segment = jnp.sum((slot_ids[:, None] >= ends[None, :]).astype(jnp.int32), axis=1)
    member = segment[:, None] == jnp.arange(count, dtype=jnp.int32)[None, :]
    offset = jnp.sum(jnp.where(member, starts[None, :], 0), axis=1)
    source = segment * LEN + slot_ids - offset
    packed = jnp.take(grads, source, axis=0)
    gathered = lax.all_gather(packed, "col", axis=1, tiled=True)
    proj_in = jnp.take(proj_in, source, axis=0)
    partial_out = jnp.dot(
        gathered,
        lax.all_gather(basis_out, "grp", axis=1, tiled=True)[0],
        preferred_element_type=jnp.float32,
    )
    proj_out = lax.psum(partial_out, "row").astype(jnp.bfloat16)
    slot_pos = jnp.arange(LEN, dtype=jnp.int32)
    total = jnp.zeros((proj_out.shape[1], proj_in.shape[1]), jnp.float32)
    padded_out = jnp.concatenate(
        [proj_out, jnp.zeros((LEN, proj_out.shape[1]), jnp.bfloat16)], axis=0
    )
    padded_in = jnp.concatenate([proj_in, jnp.zeros((LEN, proj_in.shape[1]), jnp.bfloat16)], axis=0)
    for seq in range(count):
        keep = (slot_pos < seq_lens[seq]).astype(jnp.bfloat16)
        piece_out = lax.dynamic_slice_in_dim(padded_out, starts[seq], LEN, 0)
        piece_in = lax.dynamic_slice_in_dim(padded_in, starts[seq], LEN, 0)
        total = total + outer_square(piece_out * keep[:, None], piece_in)
    summed = lax.psum(total, "grp")
    return summed / (lax.axis_size("grp") * count * LEN)


def solution(mesh):
    in_specs = (
        P("grp", "col"),
        P("grp", ("row", "col")),
        P("col", "row"),
        P("row", "grp", "col"),
        P("grp", None),
    )
    out_specs = P("col", "row")
    return jax.shard_map(
        per_device, mesh=mesh, in_specs=in_specs, out_specs=out_specs, check_vma=False
    )
```

profile of v0, /device:TPU:0, one launch (start us, length us, event | category | flops | bytes accessed | tf_op | source)
XLA Modules:
  0.0 2906.0 jit_solution(11868883489751046661)
XLA Ops:
  6.5 0.9 reduce-window.4
  7.5 0.7 fusion.13
  8.1 0.1 fusion.9
  8.2 0.1 fusion.10
  8.4 3.7 gather_fusion
  12.1 1.1 broadcast_select_fusion
  13.3 0.0 all-gather.5.cloned.1.call-start
  13.3 0.7 all-gather.5.cloned.1.call-update
  14.0 0.0 all-reduce.6.cloned.1.call-start
  14.1 0.6 fusion.17
  17.1 5.2 fusion.18
  22.2 43.5 %all-reduce.8 = bf16[192,1024]{1,0:T(8,128)(2,1)S(1)} all-reduce(f32[192,1024]{1,0:T(8,128)S(1)} %fusion.18), channel_id=1, replica_groups=mesh['grp'=4,'row'=4,'col'=2] {'col'}, use_global_device_ids=true, to_apply=%region_4.5 | all-reduce | flops 196608 | bytes 1179648 | tf_op jit(solution)/shard_map/psum | solution.py:21
  65.7 0.9 gather_fusion.1
  67.8 0.6 fusion.16
  68.4 0.6 compare_convert_fusion.2
  69.0 0.6 compare_convert_fusion.1
  69.6 0.1 broadcast_select_fusion.1
  69.7 1693.3 %all-gather.5.cloned.1.call-done = bf16[1,7168,7168]{2,1,0:T(8,128)(2,1)} async-done(((bf16[1,1792,7168]{2,1,0:T(8,128)(2,1)}), bf16[1,7168,7168]{2,1,0:T(8,128)(2,1)}) %all-gather.5.cloned.1.call-update) | async-done | bytes 102760464 | tf_op jit(solution)/shard_map/all_gather | solution.py:34
  1763.0 37.1 %fusion = f32[144,7168]{1,0:T(8,128)} fusion(bf16[144,7168]{1,0:T(8,128)(2,1)} %all-gather.3.cloned.1.call-done, bf16[1,7168,7168]{2,1,0:T(8,128)(2,1)} %all-gather.5.cloned.1.call-done), kind=kOutput, calls=%fused_computation.2 | convolution fusion | flops 14797504512 | bytes 108953600 | tf_op jit(solution)/shard_map/dot_general | solution.py:32
  1800.1 76.2 %all-reduce.7 = bf16[144,7168]{1,0:T(8,128)(2,1)} all-reduce(f32[144,7168]{1,0:T(8,128)} %fusion), channel_id=1, replica_groups=mesh['grp'=4,'row'=4,'col'=2] {'row'}, use_global_device_ids=true, to_apply=%region_3.4 | all-reduce | flops 1032192 | bytes 6193152 | tf_op jit(solution)/shard_map/psum | solution.py:37
  1876.3 13.9 fusion.3
  1890.2 19.6 multiply_add_fusion
  1909.8 966.3 %all-reduce.6.cloned.1.call-done = f32[7168,1024]{1,0:T(8,128)} async-done(((f32[7168,1024]{1,0:T(8,128)}), f32[7168,1024]{1,0:T(8,128)}) %all-reduce.6.cloned.1.call-update) | async-done | bytes 29360144 | tf_op jit(solution)/shard_map/psum | solution.py:49
  2876.1 23.3 broadcast_multiply_fusion
  (15 shorter events, 0.1 us)
Async XLA Ops:
  6.5 10.5 copy-start
  6.5 63.2 %all-gather.3.cloned.1.call-start = ((), (), s32[]{:S(2)}) async-start(), calls=%async_computation | async-start | bytes 3096576 | tf_op jit(solution)/shard_map/all_gather | solution.py:30
  13.3 0.8 copy-start.2
  13.3 1749.7 %all-gather.5.cloned.1.call-start = ((), (), s32[]{:S(2)}) async-start(), calls=%async_computation.1 | async-start | bytes 128450560 | tf_op jit(solution)/shard_map/all_gather | solution.py:34
  14.0 2862.1 %all-reduce.6.cloned.1.call-start = ((), (), s32[]{:S(2)}) async-start(), calls=%async_computation.2 | async-start | bytes 58720256 | tf_op jit(solution)/shard_map/psum | solution.py:49
  2876.1 23.3 copy-start.1
Sparse Core Ops, SparseCore 0:
  13.4 52.2 all-gather.2
  67.3 1695.6 all-gather.4
  1910.0 966.1 all-reduce.5
where the time goes:
time: 2910 us
  waiting for transfers between devices  2660 us (91%)
  blocking collectives  120 us (4%)
  matrix products  75.8 us (3%)
    all_gather x1, waiting for transfers between devices, per_device(): lax.all_gather(basis_out, 'grp', axis=1, tiled=True)[0]  1690 us
    psum x1, waiting for transfers between devices, per_device(): summed = lax.psum(total, 'grp')  966 us
    psum x1, blocking collectives, per_device(): proj_out = lax.psum(partial_out, 'row').astype(jnp.bfloat16)  76.2 us
  transfers between devices with their start and end apart: 3, of which 2 were waited for; matrix products, arithmetic and copies ran while one was open for 0% of the time, Pallas kernels for 0%

commit v1 on v0

v1 whole, which is shorter than its diff:
```python
import functools

import jax
import jax.numpy as jnp
from jax import lax
from jax.experimental import pallas as pl
from jax.experimental.pallas import tpu as pltpu
from jax.sharding import PartitionSpec as P

LEN = 96
VALID = 144
LANES = 128


def squares_kernel(groups, count, scale, left_ref, right_ref, out_ref):
    valid = left_ref.shape[0] // groups
    wide = out_ref.shape[1]
    chunk = 256 if wide % 256 == 0 else wide
    for begin in range(0, wide, chunk):
        total = None
        for group in range(groups):
            left = left_ref[pl.ds(group * valid, valid), :]
            for seq in range(count):
                right = right_ref[group * count + seq, :, pl.ds(begin, chunk)]
                block = lax.dot_general(
                    left, right, (((0,), (0,)), ((), ())), preferred_element_type=jnp.float32
                )
                total = block * block if total is None else total + block * block
        out_ref[:, pl.ds(begin, chunk)] = total * scale


def sum_of_squares(left, right, groups, count, scale):
    rows, columns = left.shape[1], right.shape[2]
    tile = rows
    for size in (512, 384, 256, 128):
        if rows % size == 0:
            tile = size
            break
    return pl.pallas_call(
        functools.partial(squares_kernel, groups, count, scale),
        grid=(rows // tile,),
        out_shape=jax.ShapeDtypeStruct((rows, columns), jnp.float32),
        in_specs=[
            pl.BlockSpec((left.shape[0], tile), lambda i: (0, i)),
            pl.BlockSpec(right.shape, lambda i: (0, 0, 0)),
        ],
        out_specs=pl.BlockSpec((tile, columns), lambda i: (i, 0)),
        cost_estimate=pl.CostEstimate(
            flops=2 * count * left.shape[0] * rows * columns,
            bytes_accessed=4 * rows * columns,
            transcendentals=0,
        ),
        compiler_params=pltpu.CompilerParams(vmem_limit_bytes=48 * 1024 * 1024),
    )(left, right)


def packing(seq_lens):
    count = seq_lens.shape[0]
    ends = jnp.cumsum(seq_lens)
    starts = ends - seq_lens
    slot_ids = jnp.arange(VALID, dtype=jnp.int32)
    segment = jnp.sum((slot_ids[:, None] >= ends[None, :]).astype(jnp.int32), axis=1)
    member = segment[:, None] == jnp.arange(count, dtype=jnp.int32)[None, :]
    offset = jnp.sum(jnp.where(member, starts[None, :], 0), axis=1)
    return segment * LEN + slot_ids - offset, segment


def per_device(acts, grads, basis_in, basis_out, lengths):
    seq_lens = lengths[0]
    count = seq_lens.shape[0]
    groups = lax.axis_size("grp")
    source, segment = packing(seq_lens)

    packed = jnp.take(grads, source, axis=0)
    gathered = lax.all_gather(packed, "col", axis=1, tiled=True)
    mine = lax.all_to_all(gathered, "grp", split_axis=1, concat_axis=0, tiled=True)
    partial_out = jnp.dot(mine, basis_out[0], preferred_element_type=jnp.float32)
    partial_out = partial_out.astype(jnp.bfloat16)

    partial_in = jnp.dot(
        jnp.take(acts, source, axis=0), basis_in, preferred_element_type=jnp.float32
    )
    proj_in = lax.psum(partial_in, "col").astype(jnp.bfloat16)
    tag = jnp.broadcast_to(segment[:, None].astype(jnp.bfloat16), (VALID, LANES))
    tagged = jnp.concatenate([proj_in, tag], axis=1)
    tagged = lax.all_gather(tagged, "grp", axis=0, tiled=False)
    every_in = tagged[:, :, : proj_in.shape[1]]
    member = tagged[:, None, :, proj_in.shape[1]] == jnp.arange(count, dtype=jnp.bfloat16)[None, :, None]
    masked = jnp.where(member[..., None], every_in[:, None], 0)
    masked = masked.reshape(groups * count, VALID, proj_in.shape[1])

    part = lax.psum_scatter(partial_out, "row", scatter_dimension=0, tiled=True)
    part = lax.psum_scatter(part, "grp", scatter_dimension=1, tiled=True)
    proj_out = lax.all_gather(part, "grp", axis=1, tiled=True)
    proj_out = lax.all_gather(proj_out, "row", axis=0, tiled=True)
    return sum_of_squares(proj_out, masked, groups, count, 1.0 / (groups * count * LEN))


def solution(mesh):
    in_specs = (
        P("grp", "col"),
        P("grp", ("row", "col")),
        P("col", "row"),
        P("row", "grp", "col"),
        P("grp", None),
    )
    out_specs = P("col", "row")
    return jax.shard_map(
        per_device, mesh=mesh, in_specs=in_specs, out_specs=out_specs, check_vma=False
    )
```

time: 2910 us -> 421 us (0.14)
  waiting for transfers between devices: 2660 us -> 257 us
  blocking collectives: 120 us -> 69.6 us
  matrix products: 75.8 us -> 26.7 us
  Pallas kernels: 0 us -> 36.6 us
    all_gather x1 -> x3, waiting for transfers between devices: 1690 us -> 108 us  [the longest x1 53.9 us: per_device(): proj_out = lax.all_gather(proj_out, 'row', axis=0, tiled=True)]
    psum x1 -> x0, waiting for transfers between devices: 966 us -> none  [per_device(): summed = lax.psum(total, 'grp')]
    reduce_scatter x0 -> x2, waiting for transfers between devices: none -> 114 us  [the longest x1 68.8 us: per_device(): part = lax.psum_scatter(partial_out, 'row', scatter_dimension=0, tiled=True)]
    psum x1 -> x0, blocking collectives: 76.2 us -> none  [per_device(): proj_out = lax.psum(partial_out, 'row').astype(jnp.bfloat16)]
    all_to_all x0 -> x1, blocking collectives: none -> 51.7 us  [per_device(): lax.all_to_all(gathered, 'grp', split_axis=1, concat_axis=0, tiled=True)]
    dot_general x4 -> x2, matrix products: 75.8 us -> 26.7 us  [the longest x1 21.9 us: per_device(): jnp.dot(mine, basis_out[0], preferred_element_type=jnp.float32)]
    pallas_call x0 -> x1, Pallas kernels: none -> 36.6 us  [sum_of_squares(): pl.pallas_call(functools.partial(squares_kernel, groups, count, scale), g...]
    all_gather x1, waiting for transfers between devices: 0.02 us -> 35.6 us  [per_device(): gathered = lax.all_gather(packed, 'col', axis=1, tiled=True)]
  transfers between devices with their start and end apart: 3 -> 6, of which waited for: 2 -> 6; matrix products, arithmetic and copies ran while one was open for 0% -> 3% of each run, Pallas kernels for 0% -> 0%
where the time goes in v1:
time: 421 us
  waiting for transfers between devices  257 us (61%)
  blocking collectives  69.6 us (17%)
  Pallas kernels  36.6 us (9%)
  matrix products  26.7 us (6%)
  between operations  13.6 us (3%)
  local copies, waits for them, and re-layouts  11 us (3%)
  other arithmetic  5.43 us (1%)
    reduce_scatter x1, waiting for transfers between devices, per_device(): part = lax.psum_scatter(partial_out, 'row', scatter_dimension=0, tiled=True)  68.8 us
    all_gather x1, waiting for transfers between devices, per_device(): proj_out = lax.all_gather(proj_out, 'row', axis=0, tiled=True)  53.9 us
    all_to_all x1, blocking collectives, per_device(): lax.all_to_all(gathered, 'grp', split_axis=1, concat_axis=0, tiled=True)  51.7 us
    reduce_scatter x1, waiting for transfers between devices, per_device(): part = lax.psum_scatter(part, 'grp', scatter_dimension=1, tiled=True)  45.4 us
    pallas_call x1, Pallas kernels, sum_of_squares(): pl.pallas_call(functools.partial(squares_kernel, groups, count, scale), g...  36.6 us
    all_gather x1, waiting for transfers between devices, per_device(): gathered = lax.all_gather(packed, 'col', axis=1, tiled=True)  35.6 us
    all_gather x1, waiting for transfers between devices, per_device(): tagged = lax.all_gather(tagged, 'grp', axis=0, tiled=False)  33 us
    dot_general x1, matrix products, per_device(): jnp.dot(mine, basis_out[0], preferred_element_type=jnp.float32)  21.9 us
  transfers between devices with their start and end apart: 6, of which 6 were waited for; matrix products, arithmetic and copies ran while one was open for 3% of the time, Pallas kernels for 0%

profile of v1, /device:TPU:0, one launch (start us, length us, event | category | flops | bytes accessed | tf_op | source)
XLA Modules:
  0.0 420.6 jit_solution(4324905027454797846)
XLA Ops:
  6.5 0.9 reduce-window.4
  7.5 0.7 fusion.11
  8.2 0.1 fusion.10
  8.4 3.7 gather_fusion
  12.1 1.1 broadcast_select_fusion
  13.3 35.6 %all-gather.6.cloned.1.call-done = bf16[144,7168]{1,0:T(8,128)(2,1)} async-done(((bf16[144,3584]{1,0:T(8,128)(2,1)}), bf16[144,7168]{1,0:T(8,128)(2,1)}) %all-gather.6.cloned.1.call-update) | async-done | bytes 2064400 | tf_op jit(solution)/shard_map/all_gather | solution.py:75
  48.9 1.7 copy.13
  50.6 51.7 %all_to_all.19 = bf16[144,4,1792]{2,0,1:T(8,128)(2,1)S(1)} all-to-all(bf16[144,4,1792]{2,0,1:T(8,128)(2,1)S(1)} %bitcast.29), channel_id=1, replica_groups=mesh['grp'=4,'row'=4,'col'=2] {'grp'}, dimensions={1} | all-to-all | bytes 4128768 | tf_op jit(solution)/shard_map/all_to_all | solution.py:76
  102.3 21.9 %fusion.2 = bf16[576,7168]{1,0:T(8,128)(2,1)} fusion(bf16[576,1792]{1,0:T(8,128)(2,1)S(1)} %bitcast.31, bf16[1,1792,7168]{2,1,0:T(8,128)(2,1)} %param.8), kind=kOutput, calls=%fused_computation.4 | convolution fusion | flops 14801633280 | bytes 36012032 | tf_op jit(solution)/shard_map/dot_general | solution.py:77
  124.3 68.8 %reduce-scatter.3.cloned.1.call-done = bf16[144,7168]{1,0:T(8,128)(2,1)} async-done(((bf16[576,7168]{1,0:T(8,128)(2,1)}), bf16[144,7168]{1,0:T(8,128)(2,1)}) %reduce-scatter.3.cloned.1.call-update) | async-done | bytes 2064400 | tf_op jit(solution)/shard_map/reduce_scatter | solution.py:92
  193.2 45.4 %reduce-scatter.5.cloned.1.call-done = bf16[144,1792]{1,0:T(8,128)(2,1)} async-done(((bf16[144,7168]{1,0:T(8,128)(2,1)}), bf16[144,1792]{1,0:T(8,128)(2,1)}) %reduce-scatter.5.cloned.1.call-update) | async-done | bytes 516112 | tf_op jit(solution)/shard_map/reduce_scatter | solution.py:93
  238.7 1.3 gather_fusion.1
  240.0 4.9 %fusion.5 = f32[144,1024]{1,0:T(8,128)S(1)} fusion(bf16[4096,1024]{1,0:T(8,128)(2,1)} %param.7, bf16[144,4096]{1,0:T(8,128)(2,1)S(1)} %gather_fusion.1, pred[144]{0:T(512)(128)(4,1)S(1)} %compare_and_fusion), kind=kOutput, calls=%fused_computation.7 | convolution fusion | flops 1208549376 | bytes 10158224 | tf_op jit(solution)/shard_map/dot_general | solution.py:80
  244.8 17.9 %all-reduce.1 = bf16[144,1024]{1,0:T(8,128)(2,1)S(1)} all-reduce(f32[144,1024]{1,0:T(8,128)S(1)} %fusion.5), channel_id=1, replica_groups=mesh['grp'=4,'row'=4,'col'=2] {'col'}, use_global_device_ids=true, to_apply=%region_5.6 | all-reduce | flops 147456 | bytes 884736 | tf_op jit(solution)/shard_map/psum | solution.py:83
  262.8 0.8 pad_maximum_fusion
  263.6 20.8 %all-gather.8.cloned.1.call-done = bf16[144,7168]{1,0:T(8,128)(2,1)} async-done(((bf16[144,1792]{1,0:T(8,128)(2,1)}), bf16[144,7168]{1,0:T(8,128)(2,1)}) %all-gather.8.cloned.1.call-update) | async-done | bytes 2064400 | tf_op jit(solution)/shard_map/all_gather | solution.py:94
  284.5 33.0 %all-gather.12.cloned.1.call-done = bf16[576,1152]{1,0:T(8,128)(2,1)} async-done(((bf16[144,1152]{1,0:T(8,128)(2,1)}), bf16[576,1152]{1,0:T(8,128)(2,1)}) %all-gather.12.cloned.1.call-update) | async-done | bytes 1327120 | tf_op jit(solution)/shard_map/all_gather | solution.py:86
  317.5 0.9 slice.12
  318.4 1.4 slice.13
  319.7 0.1 copy.10
  320.0 1.7 bitcast_select_fusion.right_ref
  321.7 53.9 %all-gather.10.cloned.1.call-done.left_ref = bf16[576,7168]{1,0:T(8,128)(2,1)} async-done(((bf16[144,7168]{1,0:T(8,128)(2,1)}), bf16[576,7168]{1,0:T(8,128)(2,1)}) %all-gather.10.cloned.1.call-update) | async-done | bytes 8257552 | tf_op jit(solution)/shard_map/all_gather | solution.py:95
  375.5 1.7 copy-done.2
  377.2 36.6 %shard_map.55 = f32[7168,1024]{1,0:T(8,128)} custom-call(bf16[576,7168]{1,0:T(8,128)(2,1)} %all-gather.10.cloned.1.call-done.left_ref, bf16[8,144,1024]{2,1,0:T(8,128)(2,1)S(1)} %copy-done.2), custom_call_target="tpu_custom_call" | custom-call | flops 16911433728 | bytes 29360128 | tf_op jit(solution)/shard_map/pallas_call | solution.py:39
  (28 shorter events, 0.7 us)
Async XLA Ops:
  6.5 232.1 %copy-start = (bf16[192,4096]{1,0:T(8,128)(2,1)S(1)}, bf16[192,4096]{1,0:T(8,128)(2,1)}, u32[]{:S(2)}) copy-start(bf16[192,4096]{1,0:T(8,128)(2,1)} %param.5) | copy-start | bytes 4718596
  6.5 42.3 %all-gather.6.cloned.1.call-start = ((), (), s32[]{:S(2)}) async-start(), calls=%async_computation.3 | async-start | bytes 3096576 | tf_op jit(solution)/shard_map/all_gather | solution.py:75
  13.3 179.8 %reduce-scatter.3.cloned.1.call-start = ((), (), s32[]{:S(2)}) async-start(), calls=%async_computation.4 | async-start | bytes 10321920 | tf_op jit(solution)/shard_map/reduce_scatter | solution.py:92
  124.2 114.4 %reduce-scatter.5.cloned.1.call-start = ((), (), s32[]{:S(2)}) async-start(), calls=%async_computation.5 | async-start | bytes 2580480 | tf_op jit(solution)/shard_map/reduce_scatter | solution.py:93
  193.1 91.3 %all-gather.8.cloned.1.call-start = ((), (), s32[]{:S(2)}) async-start(), calls=%async_computation.6 | async-start | bytes 2580480 | tf_op jit(solution)/shard_map/all_gather | solution.py:94
  238.6 78.8 %all-gather.12.cloned.1.call-start = ((), (), s32[]{:S(2)}) async-start(), calls=%async_computation.8 | async-start | bytes 1658880 | tf_op jit(solution)/shard_map/all_gather | solution.py:86
  263.6 112.0 %all-gather.10.cloned.1.call-start = ((), (), s32[]{:S(2)}) async-start(), calls=%async_computation.7 | async-start | bytes 10321920 | tf_op jit(solution)/shard_map/all_gather | solution.py:95
  375.5 1.7 copy-start.2
  377.2 36.6 %copy-start.1 = (bf16[192,4096]{1,0:T(8,128)(2,1)S(1)}, bf16[192,4096]{1,0:T(8,128)(2,1)}, u32[]{:S(2)}) copy-start(bf16[192,4096]{1,0:T(8,128)(2,1)} %param.5) | copy-start | bytes 4718596
Sparse Core Ops, SparseCore 0:
  13.4 35.4 all-gather.5
  124.3 68.7 reduce-scatter.2
  195.4 43.1 reduce-scatter.4
  240.0 44.3 all-gather.7
  285.8 31.6 all-gather.11
  318.9 56.5 all-gather.9
